TPU v7x, 128 devices: a whole 4x4x4 slice. The times are simulated.
128 devices in a mesh: row: 8 (over x, core), col: 16 (over z, y).
Axes of the slice: x: 4, y: 4, z: 4, core: 2. Of those that a mesh axis runs over, the one named last changes fastest.
Arguments:
- stored: float32 [16384, 16384], P('row', 'col'), as said below
Outputs:
- updated: float32 [16384, 16384], P('row', 'col')
- log_det: float32 [], replicated
Inputs may be any that keep to these rules, and one draw needn't show every extreme that they name: `stored`: read back into global order, the matrix is symmetric positive definite, with every eigenvalue at least 1.
All inputs are finite; a program needn't handle non-finite values.
Results may differ from a plain program's by a relative error of at most 0.0001.
Values sent between devices are 32-bit elements; how exact they have to be, the bound alone decides.
No kernel may reach another device: no remote copies, remote signals or barrier semaphores. Data moves between devices by JAX's collectives and lax.ppermute only.
A program may use at most 256 MiB of HBM per device.

v0:
```python
import jax
import jax.numpy as jnp
from jax import lax
from jax.experimental import pallas as pl
from jax.experimental.pallas import tpu as pltpu
from jax.sharding import PartitionSpec as P

NB = 512
TILE = 128
NX, NY, NZ = 4, 4, 4
HI = lax.Precision.HIGHEST
NN = (((1,), (0,)), ((), ()))
TN = (((0,), (0,)), ((), ()))
VMEM_LIMIT = 60 * 2**20


def mm(a, b, dims=NN):
    return lax.dot_general(a, b, dims, precision=HI, preferred_element_type=jnp.float32)


def device(x, core, z, y):
    return (2 * x + core) * (NZ * NY) + z * NY + y


def send(value, pairs):
    return lax.ppermute(value, ("row", "col"), pairs)


def scatter_x(chunks, ys):
    return [
        send(chunks[t], [(device(0, k, z, y), device(t, k, z, y)) for k in range(2) for z, y in ys])
        for t in range(1, NX)
    ]


def spread_y(value, cores, source):
    return [
        send(
            value,
            [(device(x, k, 0, source), device(x, k, 0, (source + t) % NY)) for x in range(NX) for k in cores],
        )
        for t in range(1, NY)
    ]


def spread_z(value, cores):
    return [
        send(
            value,
            [(device(x, k, 0, y), device(x, k, t, y)) for x in range(NX) for k in cores for y in range(NY)],
        )
        for t in range(1, NZ)
    ]


def gather_x(value, cores):
    return [value] + [
        send(
            value,
            [
                (device(x, k, z, y), device((x + t) % NX, k, z, y))
                for x in range(NX)
                for k in cores
                for z in range(NZ)
                for y in range(NY)
            ],
        )
        for t in range(1, NX)
    ]


def swap_core(value, cores):
    return send(
        value,
        [
            (device(x, k, z, y), device(x, 1 - k, z, y))
            for x in range(NX)
            for k in cores
            for z in range(NZ)
            for y in range(NY)
        ],
    )


def pick(mine, own, received):
    total = received[0]
    for other in received[1:]:
        total = total + other
    return jnp.where(mine, own, total)


def spread(x):
    return jnp.broadcast_to(x, (8, TILE))


def factor_tile(a):
    sub = lax.broadcasted_iota(jnp.int32, (8, TILE), 0)
    lane = lax.broadcasted_iota(jnp.int32, (8, TILE), 1)
    groups = TILE // 8
    rows = [a[8 * g : 8 * g + 8, :] for g in range(groups)]
    inv = [jnp.where(lane == sub + 8 * g, 1.0, 0.0).astype(jnp.float32) for g in range(groups)]
    uppers, inverses = [], []
    for b in range(groups):
        v, y = rows[b], inv[b]
        c = [spread(v[:, 8 * b + m : 8 * b + m + 1]) for m in range(8)]
        upper, inverse = jnp.zeros_like(v), jnp.zeros_like(v)
        us, ys, rs, ss = [], [], [], []
        for k in range(8):
            r = lax.rsqrt(spread(c[k][k : k + 1, :]))
            u = spread(v[k : k + 1, :]) * r
            w = spread(y[k : k + 1, :]) * r
            upper = jnp.where(sub == k, u, upper)
            inverse = jnp.where(sub == k, w, inverse)
            low = jnp.where(sub > k, c[k], 0.0) * r
            if k < 7:
                v = v - low * u
                y = y - low * w
            scaled = {}
            for m in range(k + 1, 8):
                scaled[m] = spread(c[m][k : k + 1, :]) * r
                c[m] = c[m] - low * scaled[m]
            us.append(u)
            ys.append(w)
            rs.append(r)
            ss.append(scaled)
        uppers.append(upper)
        inverses.append(inverse)
        for g in range(b + 1, groups):
            cg = [spread(rows[g][:, 8 * b + m : 8 * b + m + 1]) for m in range(8)]
            ag, wg = rows[g], inv[g]
            for k in range(8):
                low = cg[k] * rs[k]
                for m in range(k + 1, 8):
                    cg[m] = cg[m] - low * ss[k][m]
                ag = ag - low * us[k]
                wg = wg - low * ys[k]
            rows[g], inv[g] = ag, wg
    return uppers, inverses


def factor_block(work_ref, tile_ref, out_ref, log_ref):
    lane = lax.broadcasted_iota(jnp.int32, (8, TILE), 1)
    sub = lax.broadcasted_iota(jnp.int32, (8, TILE), 0)
    work_ref[:, NB:] = jnp.where(
        lax.broadcasted_iota(jnp.int32, (NB, NB), 0) == lax.broadcasted_iota(jnp.int32, (NB, NB), 1), 1.0, 0.0
    ).astype(jnp.float32)
    log_ref[...] = jnp.zeros_like(log_ref)
    out_ref[...] = jnp.zeros_like(out_ref)

    @pl.loop(0, NB // TILE)
    def _(t):
        o = pl.multiple_of(t * TILE, TILE)
        live = pl.ds(o, NB + TILE)
        uppers, inverses = factor_tile(work_ref[pl.ds(o, TILE), pl.ds(o, TILE)])
        logs = jnp.zeros((8, TILE), jnp.float32)
        for g in range(TILE // 8):
            tile_ref[8 * g : 8 * g + 8, :] = inverses[g]
            logs = logs + jnp.where(lane == sub + 8 * g, jnp.log(jnp.where(lane == sub + 8 * g, uppers[g], 1.0)), 0.0)
        log_ref[...] += logs
        out_ref[pl.ds(o, TILE), live] = mm(tile_ref[...], work_ref[pl.ds(o, TILE), live])

        @pl.loop(t + 1, NB // TILE)
        def _(i):
            q = pl.multiple_of(i * TILE, TILE)
            work_ref[pl.ds(q, TILE), live] -= mm(
                out_ref[pl.ds(o, TILE), pl.ds(q, TILE)], out_ref[pl.ds(o, TILE), live], TN
            )

        for g in range(TILE // 8):
            out_ref[pl.ds(pl.multiple_of(o + 8 * g, 8), 8), pl.ds(o, TILE)] = jnp.where(
                lane >= sub + 8 * g, uppers[g], 0.0
            )


def place_parts(dst_ref, parts_ref, x):
    for t in range(NX):
        q = lax.rem(x - t + NX, NX)
        dst_ref[:, pl.ds(pl.multiple_of(q * TILE, TILE), TILE)] = parts_ref[:, t * TILE : (t + 1) * TILE]


def first_kernel(a_ref, out_ref, log_ref, work_ref, tile_ref):
    half = NB // 2
    rows = half // (2 * NX)
    work_ref[half:, :half] = jnp.zeros((half, half), jnp.float32)
    for r in range(2 * NX):
        o = (r % 2 * NX + r // 2) * rows
        work_ref[o : o + rows, :NB] = a_ref[r * rows : (r + 1) * rows, :NB]
        work_ref[half + o : half + o + rows, half:NB] = a_ref[r * rows : (r + 1) * rows, NB:]
    factor_block(work_ref, tile_ref, out_ref, log_ref)


def second_kernel(where_ref, own_ref, other_ref, first_ref, out_ref, right_ref, log_ref, work_ref, tile_ref, sort_ref):
    x, south = where_ref[0], where_ref[1] == 0
    sort_ref[...] = jnp.where(south, own_ref[...], other_ref[...])
    place_parts(work_ref, sort_ref, x)
    right_ref[...] = mm(first_ref[:, NB:], work_ref[:, :NB])
    sort_ref[...] = jnp.where(south, other_ref[...], own_ref[...])
    place_parts(work_ref, sort_ref, x)
    work_ref[:, :NB] -= mm(right_ref[...], right_ref[...], TN)
    factor_block(work_ref, tile_ref, out_ref, log_ref)


def vmem_specs(count):
    return [pl.BlockSpec(memory_space=pltpu.VMEM)] * count


SMEM_SPEC = pl.BlockSpec(memory_space=pltpu.SMEM)


def first_block(a):
    return pl.pallas_call(
        first_kernel,
        out_shape=(jax.ShapeDtypeStruct((NB, 2 * NB), jnp.float32), jax.ShapeDtypeStruct((8, TILE), jnp.float32)),
        in_specs=vmem_specs(1),
        out_specs=vmem_specs(2),
        scratch_shapes=[pltpu.VMEM((NB, 2 * NB), jnp.float32), pltpu.VMEM((TILE, TILE), jnp.float32)],
        compiler_params=pltpu.CompilerParams(vmem_limit_bytes=VMEM_LIMIT),
        cost_estimate=pl.CostEstimate(flops=2 * 10**9, bytes_accessed=3 * 2**20, transcendentals=0),
        name="first_block",
    )(a)


def second_block(where, own, other, first):
    return pl.pallas_call(
        second_kernel,
        out_shape=(
            jax.ShapeDtypeStruct((NB, 2 * NB), jnp.float32),
            jax.ShapeDtypeStruct((NB, NB), jnp.float32),
            jax.ShapeDtypeStruct((8, TILE), jnp.float32),
        ),
        in_specs=[SMEM_SPEC] + vmem_specs(3),
        out_specs=vmem_specs(3),
        scratch_shapes=[
            pltpu.VMEM((NB, 2 * NB), jnp.float32),
            pltpu.VMEM((TILE, TILE), jnp.float32),
            pltpu.VMEM((NB, NB), jnp.float32),
        ],
        compiler_params=pltpu.CompilerParams(vmem_limit_bytes=VMEM_LIMIT),
        cost_estimate=pl.CostEstimate(flops=2 * 10**9, bytes_accessed=5 * 2**20, transcendentals=0),
        name="second_block",
    )(where, own, other, first)


def halves(value):
    high = value.astype(jnp.bfloat16)
    return high, (value - high.astype(jnp.float32)).astype(jnp.bfloat16)


def dot3(a, b):
    def dot(p, q):
        return lax.dot_general(p, q, NN, preferred_element_type=jnp.float32)

    return dot(a[0], b[0]) + (dot(a[0], b[1]) + dot(a[1], b[0]))


def solve_kernel(where_ref, *refs):
    parts, (first_ref, right_ref, second_ref, out_ref) = refs[:NX], refs[NX:]
    x, core, col = where_ref[0], where_ref[1], where_ref[2]
    sources = (first_ref[...], second_ref[...], right_ref[...])
    split = [halves(value) for value in sources + tuple(value.T for value in sources)]

    def times(n, value):
        return dot3(split[n], halves(value))

    value = jnp.concatenate([part[...] for part in parts], axis=1)
    top = times(0, value[:NB])
    bottom = times(1, value[NB:] - times(5, top))
    row = lax.broadcasted_iota(jnp.int32, (NB, TILE), 0)
    column = lax.broadcasted_iota(jnp.int32, (NB, TILE), 1)
    places, tops, bottoms = [], [], []
    first_panel, second_panel = jnp.logical_and(core == 0, col == 0), jnp.logical_and(core == 0, col == 1)
    for n in range(NX):
        place = pl.multiple_of(lax.rem(x - n + NX, NX) * TILE, TILE)
        unit = jnp.where(row == column + place, -1.0, 0.0).astype(jnp.float32)
        lanes = slice(n * TILE, (n + 1) * TILE)
        tops.append(jnp.where(first_panel, unit, jnp.where(second_panel, 0.0, top[:, lanes])))
        bottoms.append(jnp.where(second_panel, unit, jnp.where(first_panel, 0.0, bottom[:, lanes])))
        places.append(place)
    bottom = times(4, jnp.concatenate(bottoms, axis=1))
    top = times(3, jnp.concatenate(tops, axis=1) - times(2, bottom))
    for block, value in enumerate((top, bottom)):
        for n, place in enumerate(places):
            out_ref[block * NB : (block + 1) * NB, pl.ds(place, TILE)] = value[:, n * TILE : (n + 1) * TILE]


def solve(where, parts, first, right, second):
    whole = pl.BlockSpec(parts[0].shape, lambda j, w: (0, 0))
    inverse = pl.BlockSpec((NB, NB), lambda j, w: (0, 1))
    square = pl.BlockSpec((NB, NB), lambda j, w: (0, 0))
    return pl.pallas_call(
        solve_kernel,
        out_shape=jax.ShapeDtypeStruct((2 * NB, NB), jnp.float32),
        grid_spec=pltpu.PrefetchScalarGridSpec(
            num_scalar_prefetch=1,
            grid=(1,),
            in_specs=[whole] * NX + [inverse, square, inverse],
            out_specs=pl.BlockSpec((2 * NB, NB), lambda j, w: (0, 0)),
        ),
        compiler_params=pltpu.CompilerParams(vmem_limit_bytes=VMEM_LIMIT),
        cost_estimate=pl.CostEstimate(flops=3 * 10**9, bytes_accessed=7 * 2**20, transcendentals=0),
        name="solve",
    )(where, *parts, first, right, second)


def update_kernel(
    where_ref, matrix_ref, left0_ref, left1_ref, own_ref, other_ref, first_ref, second_ref, out_ref, split_ref
):
    core, col, row = where_ref[1], where_ref[2], where_ref[3]
    step = pl.program_id(0)
    rows, columns = out_ref.shape

    @pl.when(step == 0)
    def _():
        own, other = own_ref[...], other_ref[...]
        for block, value in enumerate((jnp.where(core == 0, own, other), jnp.where(core == 0, other, own))):
            lanes = slice(block * NB, (block + 1) * NB)
            high, low = halves(value)
            split_ref[: 2 * NB, lanes] = high
            split_ref[2 * NB : 4 * NB, lanes] = low
            split_ref[4 * NB :, lanes] = high

    high0, low0 = halves(left0_ref[...])
    high1, low1 = halves(left1_ref[...])
    left = jnp.concatenate([high0, high1, high0, high1, low0, low1], axis=1)
    product = lax.dot_general(left, split_ref[...], NN, preferred_element_type=jnp.float32)
    out_ref[:, NB:] = matrix_ref[:, NB:] - product[:, NB:]
    out_ref[:, :NB] = jnp.where(col < 2, 0.0, matrix_ref[:, :NB]) - product[:, :NB]

    @pl.when(jnp.logical_and(row < 2, step < NB // rows))
    def _():
        out_ref[:, NB:] = jnp.zeros((rows, columns - NB), jnp.float32)

        @pl.when(jnp.logical_not(jnp.logical_and(row == 1, col == 0)))
        def _():
            out_ref[:, :NB] = jnp.zeros((rows, NB), jnp.float32)

        @pl.when(row == col)
        def _():
            o = pl.multiple_of(step * rows, rows)
            u = jnp.where(col == 0, first_ref[:, pl.ds(o, rows)], second_ref[:, pl.ds(o, rows)])
            keep = lax.broadcasted_iota(jnp.int32, (NB, rows), 0) <= (
                lax.broadcasted_iota(jnp.int32, (NB, rows), 1) + o
            )
            out_ref[:, :NB] = jnp.where(keep, u, 0.0).T


def update(where, matrix, left, own, other, first, second):
    rows, columns = matrix.shape
    tile = 256

    def whole(value):
        return pl.BlockSpec(value.shape, lambda i, w: (0, 0))

    square = pl.BlockSpec((NB, NB), lambda i, w: (0, 0))
    return pl.pallas_call(
        update_kernel,
        out_shape=jax.ShapeDtypeStruct((rows, columns), jnp.float32),
        grid_spec=pltpu.PrefetchScalarGridSpec(
            num_scalar_prefetch=1,
            grid=(rows // tile,),
            in_specs=[
                pl.BlockSpec((tile, columns), lambda i, w: (i, 0)),
                pl.BlockSpec((tile, NB), lambda i, w: (i, 0)),
                pl.BlockSpec((tile, NB), lambda i, w: (i, 0)),
                whole(own),
                whole(other),
                square,
                square,
            ],
            out_specs=pl.BlockSpec((tile, columns), lambda i, w: (i, 0)),
            scratch_shapes=[pltpu.VMEM((6 * NB, columns), jnp.bfloat16)],
        ),
        compiler_params=pltpu.CompilerParams(vmem_limit_bytes=VMEM_LIMIT),
        cost_estimate=pl.CostEstimate(flops=12 * 10**9, bytes_accessed=28 * 2**20, transcendentals=0),
        name="update",
    )(where, matrix, *left, own, other, first, second)


def per_device(stored):
    row, col = lax.axis_index("row"), lax.axis_index("col")
    x, core = row // 2, row % 2
    z, y = col // NY, col % NY
    where = jnp.stack([x, core, col, row]).astype(jnp.int32)
    slab = stored[:, :NB]
    corner = slab[:NB]
    plane = [(zz, yy) for zz in range(NZ) for yy in range(NY)]
    both = (0, 1)

    half = NB // 2
    rows = half // (2 * NX)
    block = jnp.concatenate([corner[:half], corner[half:, half:]], axis=1)
    other = send(block[half // 2 :], [(device(0, 0, 0, 0), device(0, 1, 0, 0))])
    block = jnp.where(core == 0, block[: half // 2], other)
    chunks = [block[t * rows : (t + 1) * rows] for t in range(NX)]
    p0 = scatter_x(chunks, [(0, 0)])
    p0 = pick(x == 0, chunks[0], p0)
    p0_y = spread_y(p0, both, 0)
    left = [jnp.where(col == number, stored[:, :NB], 0.0) for number in range(2)]
    left = lax.psum(left, "col")
    p0 = pick(y == 0, p0, p0_y)
    p0_z = spread_z(p0, both)
    p0 = pick(z == 0, p0, p0_z)
    p0 = lax.all_gather(p0, "row", axis=0, tiled=True)

    strip = stored[:NB]
    chunks = [
        jnp.concatenate([strip[:, t * TILE : (t + 1) * TILE], strip[:, NB + t * TILE : NB + (t + 1) * TILE]], axis=1)
        for t in range(NX)
    ]
    quarter_x = scatter_x(chunks, plane)
    quarter = pick(x == 0, chunks[0], quarter_x)
    near, far = quarter[:, :TILE], quarter[:, TILE:]
    given = swap_core(jnp.where(core == 0, far, near), both)
    a1_y = spread_y(near, both, 1)
    a1 = pick(y == 1, near, a1_y)
    a1_z = spread_z(a1, both)
    a1 = pick(z == 0, a1, a1_z)
    a1_parts = gather_x(a1, both)
    first, log0 = first_block(p0)
    a1 = jnp.concatenate(a1_parts, axis=1)
    a1_other = swap_core(a1, both)
    kept = jnp.where(core == 0, near, far)
    right_part = jnp.where(core == 0, jnp.concatenate([kept, given], axis=0), jnp.concatenate([given, kept], axis=0))
    right_parts = gather_x(right_part, both)
    second, right, log1 = second_block(where, a1, a1_other, first)
    own = solve(where, right_parts, first, right, second)
    other = swap_core(own, both)
    matrix = update(where, stored, left, own, other, first, second)
    log_total = 2.0 * jnp.sum(log0 + log1)
    return matrix, log_total


def solution(mesh):
    return jax.shard_map(
        per_device, mesh=mesh, in_specs=(P("row", "col"),), out_specs=(P("row", "col"), P()), check_vma=False
    )
```

profile of v0, /device:TPU:0, one launch (start us, length us, event | category | flops | bytes accessed | tf_op | source)
XLA Modules:
  0.0 247.8 jit_solution(7675769852018132786)
XLA Ops:
  7.2 0.0 all-reduce.3.cloned.1.call-start
  7.2 6.9 %slice_select_fusion = (f32[2048,512]{1,0:T(8,128)}, f32[2048,512]{1,0:T(8,128)}) fusion(f32[2048,1024]{1,0:T(8,128)} %matrix_ref.1, pred[]{:T(512)S(6)} %eq.30, pred[]{:T(512)S(6)} %eq.29), kind=kLoop, calls=%fused_computation | loop fusion | flops 2097152 | bytes 12582914 | tf_op jit(solution)/shard_map/jit(_where)/select_n | solution.py:398
  14.1 0.0 all-reduce.3.cloned.1.call-update
  14.1 1.7 fusion.2
  15.9 3.5 %collective-permute-start = (f32[512,256]{1,0:T(8,128)S(1)}, f32[512,256]{1,0:T(8,128)S(1)}, u32[]{:S(2)}, u32[]{:S(2)}) collective-permute-start(f32[512,256]{1,0:T(8,128)S(1)} %pad_maximum_fusion.1), channel_id=1, source_target_pairs={{0,32},{1,33},{2,34},{3,35},{4,36},{5,37},{6,38},{7,39},{8,40},{9,... | collective-permute-start | bytes 1572872 | tf_op jit(solution)/shard_map/ppermute | solution.py:26
  19.5 2.0 collective-permute-start.2
  21.5 2.1 collective-permute-start.1
  23.6 8.1 %collective-permute-done = f32[512,256]{1,0:T(8,128)S(1)} collective-permute-done((f32[512,256]{1,0:T(8,128)S(1)}, f32[512,256]{1,0:T(8,128)S(1)}, u32[]{:S(2)}, u32[]{:S(2)}) %collective-permute-start) | collective-permute-done | bytes 524320 | tf_op jit(solution)/shard_map/ppermute | solution.py:26
  31.7 0.9 collective-permute-done.2
  32.6 9.2 %collective-permute-done.1 = f32[512,256]{1,0:T(8,128)} collective-permute-done((f32[512,256]{1,0:T(8,128)S(1)}, f32[512,256]{1,0:T(8,128)}, u32[]{:S(2)}, u32[]{:S(2)}) %collective-permute-start.1) | collective-permute-done | bytes 524320 | tf_op jit(solution)/shard_map/ppermute | solution.py:26
  41.8 1.2 maximum_select_fusion
  43.0 0.7 collective-permute-start.17
  43.7 1.3 collective-permute-start.19
  45.0 0.7 collective-permute-start.18
  45.7 1.0 slice.84
  46.7 1.1 slice.83
  47.8 1.3 collective-permute-start.7
  49.2 0.0 collective-permute-done.17
  49.2 13.0 %collective-permute-done.19 = f32[512,128]{1,0:T(8,128)S(1)} collective-permute-done((f32[512,128]{1,0:T(8,128)S(1)}, f32[512,128]{1,0:T(8,128)S(1)}, u32[]{:S(2)}, u32[]{:S(2)}) %collective-permute-start.19) | collective-permute-done | bytes 262176 | tf_op jit(solution)/shard_map/ppermute | solution.py:26
  62.2 0.1 add_select_fusion.1
  62.3 1.3 collective-permute-start.22
  63.6 1.3 collective-permute-start.21
  64.9 1.3 collective-permute-start.20
  66.3 6.0 %collective-permute-start.9 = (f32[32,768]{1,0:T(8,128)S(1)}, f32[32,768]{1,0:T(8,128)S(1)}, u32[]{:S(2)}, u32[]{:S(2)}) collective-permute-start(f32[32,768]{1,0:T(8,128)S(1)} %get-tuple-element.27), channel_id=1, source_target_pairs={{0,64},{16,80}} | collective-permute-start | bytes 294920 | tf_op jit(solution)/shard_map/ppermute | solution.py:26
  72.3 1.3 collective-permute-start.10
  73.6 1.3 collective-permute-start.8
  74.9 0.0 collective-permute-done.21
  74.9 0.0 collective-permute-done.20
  74.9 0.1 add_select_fusion
  75.0 3.0 %collective-permute-start.25 = (f32[512,128]{1,0:T(8,128)S(1)}, f32[512,128]{1,0:T(8,128)S(1)}, u32[]{:S(2)}, u32[]{:S(2)}) collective-permute-start(f32[512,128]{1,0:T(8,128)S(1)} %add_select_fusion), channel_id=1, source_target_pairs={{0,96},{1,97},{2,98},{3,99},{4,100},{5,101},{6,102},{7,103},{8,104... | collective-permute-start | bytes 786440 | tf_op jit(solution)/shard_map/ppermute | solution.py:26
  77.9 0.7 collective-permute-start.24
  78.6 0.0 collective-permute-done.9
  78.6 1.3 collective-permute-start.23
  79.9 0.0 collective-permute-done.10
  79.9 0.0 collective-permute-done.8
  80.0 19.1 %collective-permute-start.13 = (f32[32,768]{1,0:T(8,128)S(1)}, f32[32,768]{1,0:T(8,128)S(1)}, u32[]{:S(2)}, u32[]{:S(2)}) collective-permute-start(f32[32,768]{1,0:T(8,128)S(1)} %slice_select_fusion.4), channel_id=1, source_target_pairs={{0,3},{16,19},{32,35},{48,51},{64,67},{80,83},{96,99},{112,115}} | collective-permute-start | bytes 294920 | tf_op jit(solution)/shard_map/ppermute | solution.py:26
  99.0 1.3 collective-permute-start.12
  100.3 0.0 collective-permute-done.25
  100.4 1.3 collective-permute-start.11
  101.7 0.1 pad_maximum_fusion.own_ref
  101.8 0.1 collective-permute-start.26
  101.9 0.7 collective-permute-done.12
  102.5 1.3 collective-permute-done.11
  103.9 1.3 collective-permute-start.16
  105.2 1.3 collective-permute-start.15
  106.5 1.3 collective-permute-start.14
  107.8 0.1 collective-permute-start.3
  107.9 0.6 pad_add_fusion.where_ref
  108.5 2.5 %collective-permute-done.15 = f32[32,768]{1,0:T(8,128)S(1)} collective-permute-done((f32[32,768]{1,0:T(8,128)S(1)}, f32[32,768]{1,0:T(8,128)S(1)}, u32[]{:S(2)}, u32[]{:S(2)}) %collective-permute-start.15) | collective-permute-done | bytes 98336 | tf_op jit(solution)/shard_map/ppermute | solution.py:26
  111.0 2.8 %collective-permute-done.14 = f32[32,768]{1,0:T(8,128)S(1)} collective-permute-done((f32[32,768]{1,0:T(8,128)S(1)}, f32[32,768]{1,0:T(8,128)S(1)}, u32[]{:S(2)}, u32[]{:S(2)}) %collective-permute-start.14) | collective-permute-done | bytes 98336 | tf_op jit(solution)/shard_map/ppermute | solution.py:26
  113.9 1.1 collective-permute-start.6
  115.0 1.0 collective-permute-start.4
  116.0 31.6 %all_gather.3.a_ref = f32[256,768]{1,0:T(8,128)} all-gather(f32[32,768]{1,0:T(8,128)S(1)} %add_select_fusion.2), channel_id=1, replica_groups=mesh['row'=8,'col'=16] {'row'}, dimensions={0}, use_global_device_ids=true | all-gather | bytes 884736 | tf_op jit(solution)/shard_map/all_gather | solution.py:403
  147.6 23.8 %first_block.1 = (f32[512,1024]{1,0:T(8,128)}, f32[8,128]{1,0:T(8,128)}) custom-call(f32[256,768]{1,0:T(8,128)} %all_gather.3.a_ref), custom_call_target="tpu_custom_call" | custom-call | flops 2000000000 | bytes 3145728 | tf_op jit(solution)/shard_map/first_block/pallas_call | solution.py:211
  171.4 1.0 copy-done.5
  172.3 29.0 %second_block.1 = (f32[512,1024]{1,0:T(8,128)}, f32[512,512]{1,0:T(8,128)}, f32[8,128]{1,0:T(8,128)}) custom-call(s32[4]{0:T(128)} %pad_add_fusion.where_ref, f32[512,512]{1,0:T(8,128)} %copy-done, f32[512,512]{1,0:T(8,128)} %copy-done.5, f32[512,1024]{1,0:T(8,128)} %get-tuple-element.7.first_ref.refs_4_), custom_call_target="tpu_custom_call" | custom-call | flops 2000000000 | bytes 5242880 | tf_op jit(solution)/shard_map/second_block/pallas_call | solution.py:224
  201.4 0.8 copy-done.6
  202.1 0.2 copy-done.7
  202.3 10.3 %solve.1.own_ref = f32[1024,512]{1,0:T(8,128)} custom-call(s32[4]{0:T(128)} %pad_add_fusion.where_ref, f32[1024,128]{1,0:T(8,128)} %copy-done.1, f32[1024,128]{1,0:T(8,128)} %collective-permute-done.4.refs_1_, f32[1024,128]{1,0:T(8,128)} %copy-done.7, f32[1024,128]{1,0:T(8,128)} %copy-done.6, f32[512,1024]{1,0:T(8,128)} %get-tuple-element.7.first_ref.refs_4_, ...), custom_call_target="tpu_custom_call" | custom-call | flops 3000000000 | bytes 7340032 | tf_op jit(solution)/shard_map/solve/pallas_call | solution.py:290
  212.7 0.4 collective-permute-start.27
  213.0 0.6 add_reduce_fusion
  214.3 2.7 %collective-permute-done.27.other_ref = f32[1024,512]{1,0:T(8,128)S(1)} collective-permute-done((f32[1024,512]{1,0:T(8,128)}, f32[1024,512]{1,0:T(8,128)S(1)}, u32[]{:S(2)}, u32[]{:S(2)}) %collective-permute-start.27) | collective-permute-done | bytes 2097184 | tf_op jit(solution)/shard_map/ppermute | solution.py:26
  217.0 1.3 copy-done.4
  218.4 21.5 %update.1 = f32[2048,1024]{1,0:T(8,128)} custom-call(s32[4]{0:T(128)} %pad_add_fusion.where_ref, f32[2048,1024]{1,0:T(8,128)} %matrix_ref.1, f32[2048,512]{1,0:T(8,128)} %get-tuple-element.12.left0_ref, f32[2048,512]{1,0:T(8,128)} %get-tuple-element.13.left1_ref, f32[1024,512]{1,0:T(8,128)} %solve.1.own_ref, f32[1024,512]{1,0:T(8,128)} %copy-done.4, ...), custom_call_target="tpu_custom_call" | custom-call | flops 12000000000 | bytes 29360128 | tf_op jit(solution)/shard_map/update/pallas_call | solution.py:355
  (37 shorter events, 0.4 us)
Async XLA Ops:
  7.2 209.9 %all-reduce.3.cloned.1.call-start = ((), (), s32[]{:S(2)}) async-start(), calls=%async_computation | async-start | bytes 16777216 | tf_op jit(solution)/shard_map/psum | solution.py:399
  15.9 15.8 %collective-permute-start = (f32[512,256]{1,0:T(8,128)S(1)}, f32[512,256]{1,0:T(8,128)S(1)}, u32[]{:S(2)}, u32[]{:S(2)}) collective-permute-start(f32[512,256]{1,0:T(8,128)S(1)} %pad_maximum_fusion.1), channel_id=1, source_target_pairs={{0,32},{1,33},{2,34},{3,35},{4,36},{5,37},{6,38},{7,39},{8,40},{9,... | collective-permute-start | bytes 1572872 | tf_op jit(solution)/shard_map/ppermute | solution.py:26
  19.5 13.1 %collective-permute-start.2 = (f32[512,256]{1,0:T(8,128)S(1)}, f32[512,256]{1,0:T(8,128)S(1)}, u32[]{:S(2)}, u32[]{:S(2)}) collective-permute-start(f32[512,256]{1,0:T(8,128)S(1)} %pad_maximum_fusion.3), channel_id=1, source_target_pairs={{0,96},{1,97},{2,98},{3,99},{4,100},{5,101},{6,102},{7,103},{8,104... | collective-permute-start | bytes 1572872 | tf_op jit(solution)/shard_map/ppermute | solution.py:26
  21.5 20.3 %collective-permute-start.1 = (f32[512,256]{1,0:T(8,128)S(1)}, f32[512,256]{1,0:T(8,128)}, u32[]{:S(2)}, u32[]{:S(2)}) collective-permute-start(f32[512,256]{1,0:T(8,128)S(1)} %pad_maximum_fusion.2), channel_id=1, source_target_pairs={{0,64},{1,65},{2,66},{3,67},{4,68},{5,69},{6,70},{7,71},{8,72},{9,... | collective-permute-start | bytes 1572872 | tf_op jit(solution)/shard_map/ppermute | solution.py:26
  43.0 6.2 %collective-permute-start.17 = (f32[512,128]{1,0:T(8,128)S(1)}, f32[512,128]{1,0:T(8,128)S(1)}, u32[]{:S(2)}, u32[]{:S(2)}) collective-permute-start(f32[512,128]{1,0:T(8,128)S(1)} %slice.91), channel_id=1, source_target_pairs={{1,2},{17,18},{33,34},{49,50},{65,66},{81,82},{97,98},{113,114}} | collective-permute-start | bytes 786440 | tf_op jit(solution)/shard_map/ppermute | solution.py:26
  43.7 18.5 %collective-permute-start.19 = (f32[512,128]{1,0:T(8,128)S(1)}, f32[512,128]{1,0:T(8,128)S(1)}, u32[]{:S(2)}, u32[]{:S(2)}) collective-permute-start(f32[512,128]{1,0:T(8,128)S(1)} %slice.91), channel_id=1, source_target_pairs={{1,0},{17,16},{33,32},{49,48},{65,64},{81,80},{97,96},{113,112}} | collective-permute-start | bytes 786440 | tf_op jit(solution)/shard_map/ppermute | solution.py:26
  45.0 17.2 %collective-permute-start.18 = (f32[512,128]{1,0:T(8,128)S(1)}, f32[512,128]{1,0:T(8,128)S(1)}, u32[]{:S(2)}, u32[]{:S(2)}) collective-permute-start(f32[512,128]{1,0:T(8,128)S(1)} %slice.91), channel_id=1, source_target_pairs={{1,3},{17,19},{33,35},{49,51},{65,67},{81,83},{97,99},{113,115}} | collective-permute-start | bytes 786440 | tf_op jit(solution)/shard_map/ppermute | solution.py:26
  47.8 18.4 %collective-permute-start.7 = (f32[128,768]{1,0:T(8,128)S(1)}, f32[128,768]{1,0:T(8,128)S(1)}, u32[]{:S(2)}, u32[]{:S(2)}) collective-permute-start(f32[128,768]{1,0:T(8,128)S(1)} %pad_maximum_fusion.4), channel_id=1, source_target_pairs={{0,16}} | collective-permute-start | bytes 1179656 | tf_op jit(solution)/shard_map/ppermute | solution.py:26
  62.3 11.3 %collective-permute-start.22 = (f32[512,128]{1,0:T(8,128)S(1)}, f32[512,128]{1,0:T(8,128)S(1)}, u32[]{:S(2)}, u32[]{:S(2)}) collective-permute-start(f32[512,128]{1,0:T(8,128)S(1)} %get-tuple-element.24), channel_id=1, source_target_pairs={{0,12},{1,13},{2,14},{3,15},{16,28},{17,29},{18,30},{19,31},{32,44... | collective-permute-start | bytes 786440 | tf_op jit(solution)/shard_map/ppermute | solution.py:26
  63.6 11.3 %collective-permute-start.21 = (f32[512,128]{1,0:T(8,128)S(1)}, f32[512,128]{1,0:T(8,128)S(1)}, u32[]{:S(2)}, u32[]{:S(2)}) collective-permute-start(f32[512,128]{1,0:T(8,128)S(1)} %get-tuple-element.24), channel_id=1, source_target_pairs={{0,8},{1,9},{2,10},{3,11},{16,24},{17,25},{18,26},{19,27},{32,40},... | collective-permute-start | bytes 786440 | tf_op jit(solution)/shard_map/ppermute | solution.py:26
  64.9 10.0 %collective-permute-start.20 = (f32[512,128]{1,0:T(8,128)S(1)}, f32[512,128]{1,0:T(8,128)S(1)}, u32[]{:S(2)}, u32[]{:S(2)}) collective-permute-start(f32[512,128]{1,0:T(8,128)S(1)} %get-tuple-element.24), channel_id=1, source_target_pairs={{0,4},{1,5},{2,6},{3,7},{16,20},{17,21},{18,22},{19,23},{32,36},{3... | collective-permute-start | bytes 786440 | tf_op jit(solution)/shard_map/ppermute | solution.py:26
  66.3 12.3 %collective-permute-start.9 = (f32[32,768]{1,0:T(8,128)S(1)}, f32[32,768]{1,0:T(8,128)S(1)}, u32[]{:S(2)}, u32[]{:S(2)}) collective-permute-start(f32[32,768]{1,0:T(8,128)S(1)} %get-tuple-element.27), channel_id=1, source_target_pairs={{0,64},{16,80}} | collective-permute-start | bytes 294920 | tf_op jit(solution)/shard_map/ppermute | solution.py:26
  72.3 7.7 %collective-permute-start.10 = (f32[32,768]{1,0:T(8,128)S(1)}, f32[32,768]{1,0:T(8,128)S(1)}, u32[]{:S(2)}, u32[]{:S(2)}) collective-permute-start(f32[32,768]{1,0:T(8,128)S(1)} %get-tuple-element.28), channel_id=1, source_target_pairs={{0,96},{16,112}} | collective-permute-start | bytes 294920 | tf_op jit(solution)/shard_map/ppermute | solution.py:26
  73.6 6.4 %collective-permute-start.8 = (f32[32,768]{1,0:T(8,128)S(1)}, f32[32,768]{1,0:T(8,128)S(1)}, u32[]{:S(2)}, u32[]{:S(2)}) collective-permute-start(f32[32,768]{1,0:T(8,128)S(1)} %get-tuple-element.29), channel_id=1, source_target_pairs={{0,32},{16,48}} | collective-permute-start | bytes 294920 | tf_op jit(solution)/shard_map/ppermute | solution.py:26
  75.0 25.4 %collective-permute-start.25 = (f32[512,128]{1,0:T(8,128)S(1)}, f32[512,128]{1,0:T(8,128)S(1)}, u32[]{:S(2)}, u32[]{:S(2)}) collective-permute-start(f32[512,128]{1,0:T(8,128)S(1)} %add_select_fusion), channel_id=1, source_target_pairs={{0,96},{1,97},{2,98},{3,99},{4,100},{5,101},{6,102},{7,103},{8,104... | collective-permute-start | bytes 786440 | tf_op jit(solution)/shard_map/ppermute | solution.py:26
  77.9 23.7 %collective-permute-start.24 = (f32[512,128]{1,0:T(8,128)S(1)}, f32[512,128]{1,0:T(8,128)S(1)}, u32[]{:S(2)}, u32[]{:S(2)}) collective-permute-start(f32[512,128]{1,0:T(8,128)S(1)} %add_select_fusion), channel_id=1, source_target_pairs={{0,64},{1,65},{2,66},{3,67},{4,68},{5,69},{6,70},{7,71},{8,72},{9,... | collective-permute-start | bytes 786440 | tf_op jit(solution)/shard_map/ppermute | solution.py:26
  78.6 23.1 %collective-permute-start.23 = (f32[512,128]{1,0:T(8,128)S(1)}, f32[512,128]{1,0:T(8,128)S(1)}, u32[]{:S(2)}, u32[]{:S(2)}) collective-permute-start(f32[512,128]{1,0:T(8,128)S(1)} %add_select_fusion), channel_id=1, source_target_pairs={{0,32},{1,33},{2,34},{3,35},{4,36},{5,37},{6,38},{7,39},{8,40},{9,... | collective-permute-start | bytes 786440 | tf_op jit(solution)/shard_map/ppermute | solution.py:26
  80.0 21.9 %collective-permute-start.13 = (f32[32,768]{1,0:T(8,128)S(1)}, f32[32,768]{1,0:T(8,128)S(1)}, u32[]{:S(2)}, u32[]{:S(2)}) collective-permute-start(f32[32,768]{1,0:T(8,128)S(1)} %slice_select_fusion.4), channel_id=1, source_target_pairs={{0,3},{16,19},{32,35},{48,51},{64,67},{80,83},{96,99},{112,115}} | collective-permute-start | bytes 294920 | tf_op jit(solution)/shard_map/ppermute | solution.py:26
  99.0 3.5 %collective-permute-start.12 = (f32[32,768]{1,0:T(8,128)S(1)}, f32[32,768]{1,0:T(8,128)S(1)}, u32[]{:S(2)}, u32[]{:S(2)}) collective-permute-start(f32[32,768]{1,0:T(8,128)S(1)} %slice_select_fusion.4), channel_id=1, source_target_pairs={{0,2},{16,18},{32,34},{48,50},{64,66},{80,82},{96,98},{112,114}} | collective-permute-start | bytes 294920 | tf_op jit(solution)/shard_map/ppermute | solution.py:26
  100.4 3.5 %collective-permute-start.11 = (f32[32,768]{1,0:T(8,128)S(1)}, f32[32,768]{1,0:T(8,128)S(1)}, u32[]{:S(2)}, u32[]{:S(2)}) collective-permute-start(f32[32,768]{1,0:T(8,128)S(1)} %slice_select_fusion.4), channel_id=1, source_target_pairs={{0,1},{16,17},{32,33},{48,49},{64,65},{80,81},{96,97},{112,113}} | collective-permute-start | bytes 294920 | tf_op jit(solution)/shard_map/ppermute | solution.py:26
  101.8 69.6 %copy-start = (f32[512,512]{1,0:T(8,128)}, f32[512,512]{1,0:T(8,128)S(1)}, u32[]{:S(2)}) copy-start(f32[512,512]{1,0:T(8,128)S(1)} %pad_maximum_fusion.own_ref) | copy-start | bytes 3145732
  101.8 69.6 %collective-permute-start.26 = (f32[512,512]{1,0:T(8,128)S(1)}, f32[512,512]{1,0:T(8,128)S(1)}, u32[]{:S(2)}, u32[]{:S(2)}) collective-permute-start(f32[512,512]{1,0:T(8,128)S(1)} %pad_maximum_fusion.own_ref), channel_id=1, source_target_pairs={{0,16},{1,17},{2,18},{3,19},{4,20},{5,21},{6,22},{7,23},{8,24},{9,... | collective-permute-start | bytes 3145736 | tf_op jit(solution)/shard_map/ppermute | solution.py:26
  103.9 4.6 %collective-permute-start.16 = (f32[32,768]{1,0:T(8,128)S(1)}, f32[32,768]{1,0:T(8,128)S(1)}, u32[]{:S(2)}, u32[]{:S(2)}) collective-permute-start(f32[32,768]{1,0:T(8,128)S(1)} %add_select_fusion.3), channel_id=1, source_target_pairs={{0,12},{1,13},{2,14},{3,15},{16,28},{17,29},{18,30},{19,31},{32,44... | collective-permute-start | bytes 294920 | tf_op jit(solution)/shard_map/ppermute | solution.py:26
  105.2 5.8 %collective-permute-start.15 = (f32[32,768]{1,0:T(8,128)S(1)}, f32[32,768]{1,0:T(8,128)S(1)}, u32[]{:S(2)}, u32[]{:S(2)}) collective-permute-start(f32[32,768]{1,0:T(8,128)S(1)} %add_select_fusion.3), channel_id=1, source_target_pairs={{0,8},{1,9},{2,10},{3,11},{16,24},{17,25},{18,26},{19,27},{32,40},... | collective-permute-start | bytes 294920 | tf_op jit(solution)/shard_map/ppermute | solution.py:26
  106.5 7.3 %collective-permute-start.14 = (f32[32,768]{1,0:T(8,128)S(1)}, f32[32,768]{1,0:T(8,128)S(1)}, u32[]{:S(2)}, u32[]{:S(2)}) collective-permute-start(f32[32,768]{1,0:T(8,128)S(1)} %add_select_fusion.3), channel_id=1, source_target_pairs={{0,4},{1,5},{2,6},{3,7},{16,20},{17,21},{18,22},{19,23},{32,36},{3... | collective-permute-start | bytes 294920 | tf_op jit(solution)/shard_map/ppermute | solution.py:26
  107.8 6.0 %collective-permute-start.3 = (f32[512,128]{1,0:T(8,128)S(1)}, f32[512,128]{1,0:T(8,128)S(1)}, u32[]{:S(2)}, u32[]{:S(2)}) collective-permute-start(f32[512,128]{1,0:T(8,128)S(1)} %get-tuple-element.25), channel_id=1, source_target_pairs={{0,16},{1,17},{2,18},{3,19},{4,20},{5,21},{6,22},{7,23},{8,24},{9,... | collective-permute-start | bytes 786440 | tf_op jit(solution)/shard_map/ppermute | solution.py:26
  113.9 87.4 %copy-start.1 = (f32[1024,128]{1,0:T(8,128)}, f32[1024,128]{1,0:T(8,128)S(1)}, u32[]{:S(2)}) copy-start(f32[1024,128]{1,0:T(8,128)S(1)} %maximum_select_fusion.1.refs_0_) | copy-start | bytes 1572868
  113.9 87.4 %collective-permute-start.6 = (f32[1024,128]{1,0:T(8,128)S(1)}, f32[1024,128]{1,0:T(8,128)S(1)}, u32[]{:S(2)}, u32[]{:S(2)}) collective-permute-start(f32[1024,128]{1,0:T(8,128)S(1)} %maximum_select_fusion.1.refs_0_), channel_id=1, source_target_pairs={{0,96},{1,97},{2,98},{3,99},{4,100},{5,101},{6,102},{7,103},{8,104... | collective-permute-start | bytes 1572872 | tf_op jit(solution)/shard_map/ppermute | solution.py:26
  115.0 86.4 %collective-permute-start.5 = (f32[1024,128]{1,0:T(8,128)S(1)}, f32[1024,128]{1,0:T(8,128)S(1)}, u32[]{:S(2)}, u32[]{:S(2)}) collective-permute-start(f32[1024,128]{1,0:T(8,128)S(1)} %maximum_select_fusion.1.refs_0_), channel_id=1, source_target_pairs={{0,64},{1,65},{2,66},{3,67},{4,68},{5,69},{6,70},{7,71},{8,72},{9,... | collective-permute-start | bytes 1572872 | tf_op jit(solution)/shard_map/ppermute | solution.py:26
  115.0 86.4 %collective-permute-start.4 = (f32[1024,128]{1,0:T(8,128)S(1)}, f32[1024,128]{1,0:T(8,128)}, u32[]{:S(2)}, u32[]{:S(2)}) collective-permute-start(f32[1024,128]{1,0:T(8,128)S(1)} %maximum_select_fusion.1.refs_0_), channel_id=1, source_target_pairs={{0,32},{1,33},{2,34},{3,35},{4,36},{5,37},{6,38},{7,39},{8,40},{9,... | collective-permute-start | bytes 1572872 | tf_op jit(solution)/shard_map/ppermute | solution.py:26
  171.4 1.0 copy-start.5
  201.3 0.8 copy-start.6
  201.3 1.0 copy-start.7
  202.3 10.7 %copy-start.2 = (f32[8,128]{1,0:T(8,128)S(1)}, f32[8,128]{1,0:T(8,128)}, u32[]{:S(2)}) copy-start(f32[8,128]{1,0:T(8,128)} %get-tuple-element.10) | copy-start | bytes 12292
  202.3 10.7 %copy-start.3 = (f32[8,128]{1,0:T(8,128)S(1)}, f32[8,128]{1,0:T(8,128)}, u32[]{:S(2)}) copy-start(f32[8,128]{1,0:T(8,128)} %get-tuple-element.11) | copy-start | bytes 12292
  212.7 4.4 %collective-permute-start.27 = (f32[1024,512]{1,0:T(8,128)}, f32[1024,512]{1,0:T(8,128)S(1)}, u32[]{:S(2)}, u32[]{:S(2)}) collective-permute-start(f32[1024,512]{1,0:T(8,128)} %solve.1.own_ref), channel_id=1, source_target_pairs={{0,16},{1,17},{2,18},{3,19},{4,20},{5,21},{6,22},{7,23},{8,24},{9,... | collective-permute-start | bytes 6291464 | tf_op jit(solution)/shard_map/ppermute | solution.py:26
  217.0 1.3 copy-start.4
Sparse Core Ops, SparseCore 0:
  14.3 156.3 all-reduce.2
where the time goes:
time: 250 us; the launch traced here: 248 us
  Pallas kernels  84.5 us (34%)
  starting transfers between devices  57.2 us (23%)
  waiting for transfers between devices  41.3 us (17%)
  blocking collectives  31.6 us (13%)
  between operations  16.3 us (7%)
  other arithmetic  9.74 us (4%)
  local copies, waits for them, and re-layouts  7.11 us (3%)
    ppermute x28, starting transfers between devices, send(): return lax.ppermute(value, ('row', 'col'), pairs)  57.2 us
    ppermute x28, waiting for transfers between devices, send(): return lax.ppermute(value, ('row', 'col'), pairs)  41.3 us
    all_gather x1, blocking collectives, per_device(): p0 = lax.all_gather(p0, 'row', axis=0, tiled=True)  31.6 us
    pallas_call x1, Pallas kernels, second_block(): pl.pallas_call(second_kernel, out_shape=(jax.ShapeDtypeStruct((NB, 2 * NB...  29 us
    pallas_call x1, Pallas kernels, first_block(): pl.pallas_call(first_kernel, out_shape=(jax.ShapeDtypeStruct((NB, 2 * NB)...  23.8 us
    pallas_call x1, Pallas kernels, update(): pl.pallas_call(update_kernel, out_shape=jax.ShapeDtypeStruct((rows, colum...  21.5 us
    pallas_call x1, Pallas kernels, solve(): pl.pallas_call(solve_kernel, out_shape=jax.ShapeDtypeStruct((2 * NB, NB),...  10.3 us
    select_n x1, other arithmetic, per_device(): jnp.where(col == number, stored[:, :NB], 0.0)  6.9 us
  transfers between devices with their start and end apart: 29, of which 9 were waited for; matrix products, arithmetic and copies ran while one was open for 3% of the time, Pallas kernels for 25%

commit v1 on v0

--- a/solution.py
+++ b/solution.py
@@ -314,15 +314,13 @@
         own, other = own_ref[...], other_ref[...]
         for block, value in enumerate((jnp.where(core == 0, own, other), jnp.where(core == 0, other, own))):
             lanes = slice(block * NB, (block + 1) * NB)
-            high, low = halves(value)
-            split_ref[: 2 * NB, lanes] = high
-            split_ref[2 * NB : 4 * NB, lanes] = low
-            split_ref[4 * NB :, lanes] = high
-
-    high0, low0 = halves(left0_ref[...])
-    high1, low1 = halves(left1_ref[...])
-    left = jnp.concatenate([high0, high1, high0, high1, low0, low1], axis=1)
-    product = lax.dot_general(left, split_ref[...], NN, preferred_element_type=jnp.float32)
+            split_ref[0, :, lanes], split_ref[1, :, lanes] = halves(value)
+
+    def times(left_ref, half):
+        lines = pl.ds(half * NB, NB)
+        return dot3(halves(left_ref[...]), (split_ref[0, lines, :], split_ref[1, lines, :]))
+
+    product = times(left0_ref, 0) + times(left1_ref, 1)
     out_ref[:, NB:] = matrix_ref[:, NB:] - product[:, NB:]
     out_ref[:, :NB] = jnp.where(col < 2, 0.0, matrix_ref[:, :NB]) - product[:, :NB]
 
@@ -368,7 +366,7 @@
                 square,
             ],
             out_specs=pl.BlockSpec((tile, columns), lambda i, w: (i, 0)),
-            scratch_shapes=[pltpu.VMEM((6 * NB, columns), jnp.bfloat16)],
+            scratch_shapes=[pltpu.VMEM((2, 2 * NB, columns), jnp.bfloat16)],
         ),
         compiler_params=pltpu.CompilerParams(vmem_limit_bytes=VMEM_LIMIT),
         cost_estimate=pl.CostEstimate(flops=12 * 10**9, bytes_accessed=28 * 2**20, transcendentals=0),

time: 250 us -> 250 us (level)
  no operation moved by 1% of the time
where the time goes in v1:
time: 250 us; the launch traced here: 248 us
  Pallas kernels  84.4 us (34%)
  starting transfers between devices  57.2 us (23%)
  waiting for transfers between devices  41.3 us (17%)
  blocking collectives  31.6 us (13%)
  between operations  16.3 us (7%)
  other arithmetic  9.74 us (4%)
  local copies, waits for them, and re-layouts  7.11 us (3%)
    ppermute x28, starting transfers between devices, send(): return lax.ppermute(value, ('row', 'col'), pairs)  57.2 us
    ppermute x28, waiting for transfers between devices, send(): return lax.ppermute(value, ('row', 'col'), pairs)  41.3 us
    all_gather x1, blocking collectives, per_device(): p0 = lax.all_gather(p0, 'row', axis=0, tiled=True)  31.6 us
    pallas_call x1, Pallas kernels, second_block(): pl.pallas_call(second_kernel, out_shape=(jax.ShapeDtypeStruct((NB, 2 * NB...  29 us
    pallas_call x1, Pallas kernels, first_block(): pl.pallas_call(first_kernel, out_shape=(jax.ShapeDtypeStruct((NB, 2 * NB)...  23.8 us
    pallas_call x1, Pallas kernels, update(): pl.pallas_call(update_kernel, out_shape=jax.ShapeDtypeStruct((rows, colum...  21.4 us
    pallas_call x1, Pallas kernels, solve(): pl.pallas_call(solve_kernel, out_shape=jax.ShapeDtypeStruct((2 * NB, NB),...  10.3 us
    select_n x1, other arithmetic, per_device(): jnp.where(col == number, stored[:, :NB], 0.0)  6.9 us
  transfers between devices with their start and end apart: 29, of which 9 were waited for; matrix products, arithmetic and copies ran while one was open for 3% of the time, Pallas kernels for 25%

profile of v1, /device:TPU:0, one launch (start us, length us, event | category | flops | bytes accessed | tf_op | source)
XLA Modules:
  0.0 247.7 jit_solution(4659737162154239645)
XLA Ops:
  7.2 0.0 all-reduce.3.cloned.1.call-start
  7.2 6.9 %slice_select_fusion = (f32[2048,512]{1,0:T(8,128)}, f32[2048,512]{1,0:T(8,128)}) fusion(f32[2048,1024]{1,0:T(8,128)} %matrix_ref.1, pred[]{:T(512)S(6)} %eq.30, pred[]{:T(512)S(6)} %eq.29), kind=kLoop, calls=%fused_computation | loop fusion | flops 2097152 | bytes 12582914 | tf_op jit(solution)/shard_map/jit(_where)/select_n | solution.py:396
  14.1 0.0 all-reduce.3.cloned.1.call-update
  14.1 1.7 fusion.2
  15.9 3.5 %collective-permute-start = (f32[512,256]{1,0:T(8,128)S(1)}, f32[512,256]{1,0:T(8,128)S(1)}, u32[]{:S(2)}, u32[]{:S(2)}) collective-permute-start(f32[512,256]{1,0:T(8,128)S(1)} %pad_maximum_fusion.1), channel_id=1, source_target_pairs={{0,32},{1,33},{2,34},{3,35},{4,36},{5,37},{6,38},{7,39},{8,40},{9,... | collective-permute-start | bytes 1572872 | tf_op jit(solution)/shard_map/ppermute | solution.py:26
  19.5 2.0 collective-permute-start.2
  21.5 2.1 collective-permute-start.1
  23.6 8.1 %collective-permute-done = f32[512,256]{1,0:T(8,128)S(1)} collective-permute-done((f32[512,256]{1,0:T(8,128)S(1)}, f32[512,256]{1,0:T(8,128)S(1)}, u32[]{:S(2)}, u32[]{:S(2)}) %collective-permute-start) | collective-permute-done | bytes 524320 | tf_op jit(solution)/shard_map/ppermute | solution.py:26
  31.7 0.9 collective-permute-done.2
  32.6 9.2 %collective-permute-done.1 = f32[512,256]{1,0:T(8,128)} collective-permute-done((f32[512,256]{1,0:T(8,128)S(1)}, f32[512,256]{1,0:T(8,128)}, u32[]{:S(2)}, u32[]{:S(2)}) %collective-permute-start.1) | collective-permute-done | bytes 524320 | tf_op jit(solution)/shard_map/ppermute | solution.py:26
  41.8 1.2 maximum_select_fusion
  43.0 0.7 collective-permute-start.17
  43.7 1.3 collective-permute-start.19
  45.0 0.7 collective-permute-start.18
  45.7 1.0 slice.84
  46.7 1.1 slice.83
  47.8 1.3 collective-permute-start.7
  49.2 0.0 collective-permute-done.17
  49.2 13.0 %collective-permute-done.19 = f32[512,128]{1,0:T(8,128)S(1)} collective-permute-done((f32[512,128]{1,0:T(8,128)S(1)}, f32[512,128]{1,0:T(8,128)S(1)}, u32[]{:S(2)}, u32[]{:S(2)}) %collective-permute-start.19) | collective-permute-done | bytes 262176 | tf_op jit(solution)/shard_map/ppermute | solution.py:26
  62.2 0.1 add_select_fusion.1
  62.3 1.3 collective-permute-start.22
  63.6 1.3 collective-permute-start.21
  64.9 1.3 collective-permute-start.20
  66.3 6.0 %collective-permute-start.9 = (f32[32,768]{1,0:T(8,128)S(1)}, f32[32,768]{1,0:T(8,128)S(1)}, u32[]{:S(2)}, u32[]{:S(2)}) collective-permute-start(f32[32,768]{1,0:T(8,128)S(1)} %get-tuple-element.27), channel_id=1, source_target_pairs={{0,64},{16,80}} | collective-permute-start | bytes 294920 | tf_op jit(solution)/shard_map/ppermute | solution.py:26
  72.3 1.3 collective-permute-start.10
  73.6 1.3 collective-permute-start.8
  74.9 0.0 collective-permute-done.21
  74.9 0.0 collective-permute-done.20
  74.9 0.1 add_select_fusion
  75.0 3.0 %collective-permute-start.25 = (f32[512,128]{1,0:T(8,128)S(1)}, f32[512,128]{1,0:T(8,128)S(1)}, u32[]{:S(2)}, u32[]{:S(2)}) collective-permute-start(f32[512,128]{1,0:T(8,128)S(1)} %add_select_fusion), channel_id=1, source_target_pairs={{0,96},{1,97},{2,98},{3,99},{4,100},{5,101},{6,102},{7,103},{8,104... | collective-permute-start | bytes 786440 | tf_op jit(solution)/shard_map/ppermute | solution.py:26
  77.9 0.7 collective-permute-start.24
  78.6 0.0 collective-permute-done.9
  78.6 1.3 collective-permute-start.23
  79.9 0.0 collective-permute-done.10
  79.9 0.0 collective-permute-done.8
  80.0 19.1 %collective-permute-start.13 = (f32[32,768]{1,0:T(8,128)S(1)}, f32[32,768]{1,0:T(8,128)S(1)}, u32[]{:S(2)}, u32[]{:S(2)}) collective-permute-start(f32[32,768]{1,0:T(8,128)S(1)} %slice_select_fusion.4), channel_id=1, source_target_pairs={{0,3},{16,19},{32,35},{48,51},{64,67},{80,83},{96,99},{112,115}} | collective-permute-start | bytes 294920 | tf_op jit(solution)/shard_map/ppermute | solution.py:26
  99.0 1.3 collective-permute-start.12
  100.3 0.0 collective-permute-done.25
  100.4 1.3 collective-permute-start.11
  101.7 0.1 pad_maximum_fusion.own_ref
  101.8 0.1 collective-permute-start.26
  101.9 0.7 collective-permute-done.12
  102.5 1.3 collective-permute-done.11
  103.9 1.3 collective-permute-start.16
  105.2 1.3 collective-permute-start.15
  106.5 1.3 collective-permute-start.14
  107.8 0.1 collective-permute-start.3
  107.9 0.6 pad_add_fusion.where_ref
  108.5 2.5 %collective-permute-done.15 = f32[32,768]{1,0:T(8,128)S(1)} collective-permute-done((f32[32,768]{1,0:T(8,128)S(1)}, f32[32,768]{1,0:T(8,128)S(1)}, u32[]{:S(2)}, u32[]{:S(2)}) %collective-permute-start.15) | collective-permute-done | bytes 98336 | tf_op jit(solution)/shard_map/ppermute | solution.py:26
  111.0 2.8 %collective-permute-done.14 = f32[32,768]{1,0:T(8,128)S(1)} collective-permute-done((f32[32,768]{1,0:T(8,128)S(1)}, f32[32,768]{1,0:T(8,128)S(1)}, u32[]{:S(2)}, u32[]{:S(2)}) %collective-permute-start.14) | collective-permute-done | bytes 98336 | tf_op jit(solution)/shard_map/ppermute | solution.py:26
  113.9 1.1 collective-permute-start.6
  115.0 1.0 collective-permute-start.4
  116.0 31.6 %all_gather.3.a_ref = f32[256,768]{1,0:T(8,128)} all-gather(f32[32,768]{1,0:T(8,128)S(1)} %add_select_fusion.2), channel_id=1, replica_groups=mesh['row'=8,'col'=16] {'row'}, dimensions={0}, use_global_device_ids=true | all-gather | bytes 884736 | tf_op jit(solution)/shard_map/all_gather | solution.py:401
  147.6 23.8 %first_block.1 = (f32[512,1024]{1,0:T(8,128)}, f32[8,128]{1,0:T(8,128)}) custom-call(f32[256,768]{1,0:T(8,128)} %all_gather.3.a_ref), custom_call_target="tpu_custom_call" | custom-call | flops 2000000000 | bytes 3145728 | tf_op jit(solution)/shard_map/first_block/pallas_call | solution.py:211
  171.4 1.0 copy-done.5
  172.3 29.0 %second_block.1 = (f32[512,1024]{1,0:T(8,128)}, f32[512,512]{1,0:T(8,128)}, f32[8,128]{1,0:T(8,128)}) custom-call(s32[4]{0:T(128)} %pad_add_fusion.where_ref, f32[512,512]{1,0:T(8,128)} %copy-done, f32[512,512]{1,0:T(8,128)} %copy-done.5, f32[512,1024]{1,0:T(8,128)} %get-tuple-element.7.first_ref.refs_4_), custom_call_target="tpu_custom_call" | custom-call | flops 2000000000 | bytes 5242880 | tf_op jit(solution)/shard_map/second_block/pallas_call | solution.py:224
  201.4 0.8 copy-done.6
  202.1 0.2 copy-done.7
  202.3 10.3 %solve.1.own_ref = f32[1024,512]{1,0:T(8,128)} custom-call(s32[4]{0:T(128)} %pad_add_fusion.where_ref, f32[1024,128]{1,0:T(8,128)} %copy-done.1, f32[1024,128]{1,0:T(8,128)} %collective-permute-done.4.refs_1_, f32[1024,128]{1,0:T(8,128)} %copy-done.7, f32[1024,128]{1,0:T(8,128)} %copy-done.6, f32[512,1024]{1,0:T(8,128)} %get-tuple-element.7.first_ref.refs_4_, ...), custom_call_target="tpu_custom_call" | custom-call | flops 3000000000 | bytes 7340032 | tf_op jit(solution)/shard_map/solve/pallas_call | solution.py:290
  212.7 0.4 collective-permute-start.27
  213.0 0.6 add_reduce_fusion
  214.3 2.7 %collective-permute-done.27.other_ref = f32[1024,512]{1,0:T(8,128)S(1)} collective-permute-done((f32[1024,512]{1,0:T(8,128)}, f32[1024,512]{1,0:T(8,128)S(1)}, u32[]{:S(2)}, u32[]{:S(2)}) %collective-permute-start.27) | collective-permute-done | bytes 2097184 | tf_op jit(solution)/shard_map/ppermute | solution.py:26
  217.0 1.3 copy-done.4
  218.4 21.4 %update.1 = f32[2048,1024]{1,0:T(8,128)} custom-call(s32[4]{0:T(128)} %pad_add_fusion.where_ref, f32[2048,1024]{1,0:T(8,128)} %matrix_ref.1, f32[2048,512]{1,0:T(8,128)} %get-tuple-element.12.left0_ref, f32[2048,512]{1,0:T(8,128)} %get-tuple-element.13.left1_ref, f32[1024,512]{1,0:T(8,128)} %solve.1.own_ref, f32[1024,512]{1,0:T(8,128)} %copy-done.4, ...), custom_call_target="tpu_custom_call" | custom-call | flops 12000000000 | bytes 29360128 | tf_op jit(solution)/shard_map/update/pallas_call | solution.py:353
  (37 shorter events, 0.4 us)
Async XLA Ops:
  7.2 209.9 %all-reduce.3.cloned.1.call-start = ((), (), s32[]{:S(2)}) async-start(), calls=%async_computation | async-start | bytes 16777216 | tf_op jit(solution)/shard_map/psum | solution.py:397
  15.9 15.8 %collective-permute-start = (f32[512,256]{1,0:T(8,128)S(1)}, f32[512,256]{1,0:T(8,128)S(1)}, u32[]{:S(2)}, u32[]{:S(2)}) collective-permute-start(f32[512,256]{1,0:T(8,128)S(1)} %pad_maximum_fusion.1), channel_id=1, source_target_pairs={{0,32},{1,33},{2,34},{3,35},{4,36},{5,37},{6,38},{7,39},{8,40},{9,... | collective-permute-start | bytes 1572872 | tf_op jit(solution)/shard_map/ppermute | solution.py:26
  19.5 13.1 %collective-permute-start.2 = (f32[512,256]{1,0:T(8,128)S(1)}, f32[512,256]{1,0:T(8,128)S(1)}, u32[]{:S(2)}, u32[]{:S(2)}) collective-permute-start(f32[512,256]{1,0:T(8,128)S(1)} %pad_maximum_fusion.3), channel_id=1, source_target_pairs={{0,96},{1,97},{2,98},{3,99},{4,100},{5,101},{6,102},{7,103},{8,104... | collective-permute-start | bytes 1572872 | tf_op jit(solution)/shard_map/ppermute | solution.py:26
  21.5 20.3 %collective-permute-start.1 = (f32[512,256]{1,0:T(8,128)S(1)}, f32[512,256]{1,0:T(8,128)}, u32[]{:S(2)}, u32[]{:S(2)}) collective-permute-start(f32[512,256]{1,0:T(8,128)S(1)} %pad_maximum_fusion.2), channel_id=1, source_target_pairs={{0,64},{1,65},{2,66},{3,67},{4,68},{5,69},{6,70},{7,71},{8,72},{9,... | collective-permute-start | bytes 1572872 | tf_op jit(solution)/shard_map/ppermute | solution.py:26
  43.0 6.2 %collective-permute-start.17 = (f32[512,128]{1,0:T(8,128)S(1)}, f32[512,128]{1,0:T(8,128)S(1)}, u32[]{:S(2)}, u32[]{:S(2)}) collective-permute-start(f32[512,128]{1,0:T(8,128)S(1)} %slice.91), channel_id=1, source_target_pairs={{1,2},{17,18},{33,34},{49,50},{65,66},{81,82},{97,98},{113,114}} | collective-permute-start | bytes 786440 | tf_op jit(solution)/shard_map/ppermute | solution.py:26
  43.7 18.5 %collective-permute-start.19 = (f32[512,128]{1,0:T(8,128)S(1)}, f32[512,128]{1,0:T(8,128)S(1)}, u32[]{:S(2)}, u32[]{:S(2)}) collective-permute-start(f32[512,128]{1,0:T(8,128)S(1)} %slice.91), channel_id=1, source_target_pairs={{1,0},{17,16},{33,32},{49,48},{65,64},{81,80},{97,96},{113,112}} | collective-permute-start | bytes 786440 | tf_op jit(solution)/shard_map/ppermute | solution.py:26
  45.0 17.2 %collective-permute-start.18 = (f32[512,128]{1,0:T(8,128)S(1)}, f32[512,128]{1,0:T(8,128)S(1)}, u32[]{:S(2)}, u32[]{:S(2)}) collective-permute-start(f32[512,128]{1,0:T(8,128)S(1)} %slice.91), channel_id=1, source_target_pairs={{1,3},{17,19},{33,35},{49,51},{65,67},{81,83},{97,99},{113,115}} | collective-permute-start | bytes 786440 | tf_op jit(solution)/shard_map/ppermute | solution.py:26
  47.8 18.4 %collective-permute-start.7 = (f32[128,768]{1,0:T(8,128)S(1)}, f32[128,768]{1,0:T(8,128)S(1)}, u32[]{:S(2)}, u32[]{:S(2)}) collective-permute-start(f32[128,768]{1,0:T(8,128)S(1)} %pad_maximum_fusion.4), channel_id=1, source_target_pairs={{0,16}} | collective-permute-start | bytes 1179656 | tf_op jit(solution)/shard_map/ppermute | solution.py:26
  62.3 11.3 %collective-permute-start.22 = (f32[512,128]{1,0:T(8,128)S(1)}, f32[512,128]{1,0:T(8,128)S(1)}, u32[]{:S(2)}, u32[]{:S(2)}) collective-permute-start(f32[512,128]{1,0:T(8,128)S(1)} %get-tuple-element.24), channel_id=1, source_target_pairs={{0,12},{1,13},{2,14},{3,15},{16,28},{17,29},{18,30},{19,31},{32,44... | collective-permute-start | bytes 786440 | tf_op jit(solution)/shard_map/ppermute | solution.py:26
  63.6 11.3 %collective-permute-start.21 = (f32[512,128]{1,0:T(8,128)S(1)}, f32[512,128]{1,0:T(8,128)S(1)}, u32[]{:S(2)}, u32[]{:S(2)}) collective-permute-start(f32[512,128]{1,0:T(8,128)S(1)} %get-tuple-element.24), channel_id=1, source_target_pairs={{0,8},{1,9},{2,10},{3,11},{16,24},{17,25},{18,26},{19,27},{32,40},... | collective-permute-start | bytes 786440 | tf_op jit(solution)/shard_map/ppermute | solution.py:26
  64.9 10.0 %collective-permute-start.20 = (f32[512,128]{1,0:T(8,128)S(1)}, f32[512,128]{1,0:T(8,128)S(1)}, u32[]{:S(2)}, u32[]{:S(2)}) collective-permute-start(f32[512,128]{1,0:T(8,128)S(1)} %get-tuple-element.24), channel_id=1, source_target_pairs={{0,4},{1,5},{2,6},{3,7},{16,20},{17,21},{18,22},{19,23},{32,36},{3... | collective-permute-start | bytes 786440 | tf_op jit(solution)/shard_map/ppermute | solution.py:26
  66.3 12.3 %collective-permute-start.9 = (f32[32,768]{1,0:T(8,128)S(1)}, f32[32,768]{1,0:T(8,128)S(1)}, u32[]{:S(2)}, u32[]{:S(2)}) collective-permute-start(f32[32,768]{1,0:T(8,128)S(1)} %get-tuple-element.27), channel_id=1, source_target_pairs={{0,64},{16,80}} | collective-permute-start | bytes 294920 | tf_op jit(solution)/shard_map/ppermute | solution.py:26
  72.3 7.7 %collective-permute-start.10 = (f32[32,768]{1,0:T(8,128)S(1)}, f32[32,768]{1,0:T(8,128)S(1)}, u32[]{:S(2)}, u32[]{:S(2)}) collective-permute-start(f32[32,768]{1,0:T(8,128)S(1)} %get-tuple-element.28), channel_id=1, source_target_pairs={{0,96},{16,112}} | collective-permute-start | bytes 294920 | tf_op jit(solution)/shard_map/ppermute | solution.py:26
  73.6 6.4 %collective-permute-start.8 = (f32[32,768]{1,0:T(8,128)S(1)}, f32[32,768]{1,0:T(8,128)S(1)}, u32[]{:S(2)}, u32[]{:S(2)}) collective-permute-start(f32[32,768]{1,0:T(8,128)S(1)} %get-tuple-element.29), channel_id=1, source_target_pairs={{0,32},{16,48}} | collective-permute-start | bytes 294920 | tf_op jit(solution)/shard_map/ppermute | solution.py:26
  75.0 25.4 %collective-permute-start.25 = (f32[512,128]{1,0:T(8,128)S(1)}, f32[512,128]{1,0:T(8,128)S(1)}, u32[]{:S(2)}, u32[]{:S(2)}) collective-permute-start(f32[512,128]{1,0:T(8,128)S(1)} %add_select_fusion), channel_id=1, source_target_pairs={{0,96},{1,97},{2,98},{3,99},{4,100},{5,101},{6,102},{7,103},{8,104... | collective-permute-start | bytes 786440 | tf_op jit(solution)/shard_map/ppermute | solution.py:26
  77.9 23.7 %collective-permute-start.24 = (f32[512,128]{1,0:T(8,128)S(1)}, f32[512,128]{1,0:T(8,128)S(1)}, u32[]{:S(2)}, u32[]{:S(2)}) collective-permute-start(f32[512,128]{1,0:T(8,128)S(1)} %add_select_fusion), channel_id=1, source_target_pairs={{0,64},{1,65},{2,66},{3,67},{4,68},{5,69},{6,70},{7,71},{8,72},{9,... | collective-permute-start | bytes 786440 | tf_op jit(solution)/shard_map/ppermute | solution.py:26
  78.6 23.1 %collective-permute-start.23 = (f32[512,128]{1,0:T(8,128)S(1)}, f32[512,128]{1,0:T(8,128)S(1)}, u32[]{:S(2)}, u32[]{:S(2)}) collective-permute-start(f32[512,128]{1,0:T(8,128)S(1)} %add_select_fusion), channel_id=1, source_target_pairs={{0,32},{1,33},{2,34},{3,35},{4,36},{5,37},{6,38},{7,39},{8,40},{9,... | collective-permute-start | bytes 786440 | tf_op jit(solution)/shard_map/ppermute | solution.py:26
  80.0 21.9 %collective-permute-start.13 = (f32[32,768]{1,0:T(8,128)S(1)}, f32[32,768]{1,0:T(8,128)S(1)}, u32[]{:S(2)}, u32[]{:S(2)}) collective-permute-start(f32[32,768]{1,0:T(8,128)S(1)} %slice_select_fusion.4), channel_id=1, source_target_pairs={{0,3},{16,19},{32,35},{48,51},{64,67},{80,83},{96,99},{112,115}} | collective-permute-start | bytes 294920 | tf_op jit(solution)/shard_map/ppermute | solution.py:26
  99.0 3.5 %collective-permute-start.12 = (f32[32,768]{1,0:T(8,128)S(1)}, f32[32,768]{1,0:T(8,128)S(1)}, u32[]{:S(2)}, u32[]{:S(2)}) collective-permute-start(f32[32,768]{1,0:T(8,128)S(1)} %slice_select_fusion.4), channel_id=1, source_target_pairs={{0,2},{16,18},{32,34},{48,50},{64,66},{80,82},{96,98},{112,114}} | collective-permute-start | bytes 294920 | tf_op jit(solution)/shard_map/ppermute | solution.py:26
  100.4 3.5 %collective-permute-start.11 = (f32[32,768]{1,0:T(8,128)S(1)}, f32[32,768]{1,0:T(8,128)S(1)}, u32[]{:S(2)}, u32[]{:S(2)}) collective-permute-start(f32[32,768]{1,0:T(8,128)S(1)} %slice_select_fusion.4), channel_id=1, source_target_pairs={{0,1},{16,17},{32,33},{48,49},{64,65},{80,81},{96,97},{112,113}} | collective-permute-start | bytes 294920 | tf_op jit(solution)/shard_map/ppermute | solution.py:26
  101.8 69.6 %copy-start = (f32[512,512]{1,0:T(8,128)}, f32[512,512]{1,0:T(8,128)S(1)}, u32[]{:S(2)}) copy-start(f32[512,512]{1,0:T(8,128)S(1)} %pad_maximum_fusion.own_ref) | copy-start | bytes 3145732
  101.8 69.6 %collective-permute-start.26 = (f32[512,512]{1,0:T(8,128)S(1)}, f32[512,512]{1,0:T(8,128)S(1)}, u32[]{:S(2)}, u32[]{:S(2)}) collective-permute-start(f32[512,512]{1,0:T(8,128)S(1)} %pad_maximum_fusion.own_ref), channel_id=1, source_target_pairs={{0,16},{1,17},{2,18},{3,19},{4,20},{5,21},{6,22},{7,23},{8,24},{9,... | collective-permute-start | bytes 3145736 | tf_op jit(solution)/shard_map/ppermute | solution.py:26
  103.9 4.6 %collective-permute-start.16 = (f32[32,768]{1,0:T(8,128)S(1)}, f32[32,768]{1,0:T(8,128)S(1)}, u32[]{:S(2)}, u32[]{:S(2)}) collective-permute-start(f32[32,768]{1,0:T(8,128)S(1)} %add_select_fusion.3), channel_id=1, source_target_pairs={{0,12},{1,13},{2,14},{3,15},{16,28},{17,29},{18,30},{19,31},{32,44... | collective-permute-start | bytes 294920 | tf_op jit(solution)/shard_map/ppermute | solution.py:26
  105.2 5.8 %collective-permute-start.15 = (f32[32,768]{1,0:T(8,128)S(1)}, f32[32,768]{1,0:T(8,128)S(1)}, u32[]{:S(2)}, u32[]{:S(2)}) collective-permute-start(f32[32,768]{1,0:T(8,128)S(1)} %add_select_fusion.3), channel_id=1, source_target_pairs={{0,8},{1,9},{2,10},{3,11},{16,24},{17,25},{18,26},{19,27},{32,40},... | collective-permute-start | bytes 294920 | tf_op jit(solution)/shard_map/ppermute | solution.py:26
  106.5 7.3 %collective-permute-start.14 = (f32[32,768]{1,0:T(8,128)S(1)}, f32[32,768]{1,0:T(8,128)S(1)}, u32[]{:S(2)}, u32[]{:S(2)}) collective-permute-start(f32[32,768]{1,0:T(8,128)S(1)} %add_select_fusion.3), channel_id=1, source_target_pairs={{0,4},{1,5},{2,6},{3,7},{16,20},{17,21},{18,22},{19,23},{32,36},{3... | collective-permute-start | bytes 294920 | tf_op jit(solution)/shard_map/ppermute | solution.py:26
  107.8 6.0 %collective-permute-start.3 = (f32[512,128]{1,0:T(8,128)S(1)}, f32[512,128]{1,0:T(8,128)S(1)}, u32[]{:S(2)}, u32[]{:S(2)}) collective-permute-start(f32[512,128]{1,0:T(8,128)S(1)} %get-tuple-element.25), channel_id=1, source_target_pairs={{0,16},{1,17},{2,18},{3,19},{4,20},{5,21},{6,22},{7,23},{8,24},{9,... | collective-permute-start | bytes 786440 | tf_op jit(solution)/shard_map/ppermute | solution.py:26
  113.9 87.4 %copy-start.1 = (f32[1024,128]{1,0:T(8,128)}, f32[1024,128]{1,0:T(8,128)S(1)}, u32[]{:S(2)}) copy-start(f32[1024,128]{1,0:T(8,128)S(1)} %maximum_select_fusion.1.refs_0_) | copy-start | bytes 1572868
  113.9 87.4 %collective-permute-start.6 = (f32[1024,128]{1,0:T(8,128)S(1)}, f32[1024,128]{1,0:T(8,128)S(1)}, u32[]{:S(2)}, u32[]{:S(2)}) collective-permute-start(f32[1024,128]{1,0:T(8,128)S(1)} %maximum_select_fusion.1.refs_0_), channel_id=1, source_target_pairs={{0,96},{1,97},{2,98},{3,99},{4,100},{5,101},{6,102},{7,103},{8,104... | collective-permute-start | bytes 1572872 | tf_op jit(solution)/shard_map/ppermute | solution.py:26
  115.0 86.4 %collective-permute-start.5 = (f32[1024,128]{1,0:T(8,128)S(1)}, f32[1024,128]{1,0:T(8,128)S(1)}, u32[]{:S(2)}, u32[]{:S(2)}) collective-permute-start(f32[1024,128]{1,0:T(8,128)S(1)} %maximum_select_fusion.1.refs_0_), channel_id=1, source_target_pairs={{0,64},{1,65},{2,66},{3,67},{4,68},{5,69},{6,70},{7,71},{8,72},{9,... | collective-permute-start | bytes 1572872 | tf_op jit(solution)/shard_map/ppermute | solution.py:26
  115.0 86.4 %collective-permute-start.4 = (f32[1024,128]{1,0:T(8,128)S(1)}, f32[1024,128]{1,0:T(8,128)}, u32[]{:S(2)}, u32[]{:S(2)}) collective-permute-start(f32[1024,128]{1,0:T(8,128)S(1)} %maximum_select_fusion.1.refs_0_), channel_id=1, source_target_pairs={{0,32},{1,33},{2,34},{3,35},{4,36},{5,37},{6,38},{7,39},{8,40},{9,... | collective-permute-start | bytes 1572872 | tf_op jit(solution)/shard_map/ppermute | solution.py:26
  171.4 1.0 copy-start.5
  201.3 0.8 copy-start.6
  201.3 1.0 copy-start.7
  202.3 10.7 %copy-start.2 = (f32[8,128]{1,0:T(8,128)S(1)}, f32[8,128]{1,0:T(8,128)}, u32[]{:S(2)}) copy-start(f32[8,128]{1,0:T(8,128)} %get-tuple-element.10) | copy-start | bytes 12292
  202.3 10.7 %copy-start.3 = (f32[8,128]{1,0:T(8,128)S(1)}, f32[8,128]{1,0:T(8,128)}, u32[]{:S(2)}) copy-start(f32[8,128]{1,0:T(8,128)} %get-tuple-element.11) | copy-start | bytes 12292
  212.7 4.4 %collective-permute-start.27 = (f32[1024,512]{1,0:T(8,128)}, f32[1024,512]{1,0:T(8,128)S(1)}, u32[]{:S(2)}, u32[]{:S(2)}) collective-permute-start(f32[1024,512]{1,0:T(8,128)} %solve.1.own_ref), channel_id=1, source_target_pairs={{0,16},{1,17},{2,18},{3,19},{4,20},{5,21},{6,22},{7,23},{8,24},{9,... | collective-permute-start | bytes 6291464 | tf_op jit(solution)/shard_map/ppermute | solution.py:26
  217.0 1.3 copy-start.4
Sparse Core Ops, SparseCore 0:
  14.3 156.3 all-reduce.2
